TPU v7x, 256 devices: a whole 4x4x8 slice. The times are simulated.
256 devices in a mesh: row: 8 (over y, z_lo), col: 8 (over z_hi, core), layer: 4 (over x).
Axes of the slice: x: 4, y: 4, z: 8 (z_hi: 4, z_lo: 2; z = z_hi * 2 + z_lo), core: 2. Of those that a mesh axis runs over, the one named last changes fastest.
Arguments:
- density_tiles: bfloat16 [192, 8, 2, 128, 128], P(('row', 'col')), may hold values from -1.5 to 1.5
- tile_columns: int32 [192, 8, 2], P(('row', 'col')), may hold values from -1 to 191, as said below
Outputs:
- square_tiles: bfloat16 [192, 8, 2, 128, 128], P(('row', 'col'), None, None, 'layer')
Inputs may be any that keep to these rules, and one draw needn't show every extreme that they name: `tile_columns`: entry [i, g, s] is a tile column in group g (columns g * 24 to (g + 1) * 24 - 1) or -1; within one block row and group the listed columns are distinct and empty slots come after the listed ones; block row i lists its own column i in the first slot of its group, whose 2 slots are all listed; other groups hold 0 to 2 listed tiles.
All inputs are finite; a program needn't handle non-finite values.
Results may differ from a plain program's by a relative error of at most 0.0048.
Values may be sent and summed in bfloat16 or wider, within the bound.
No kernel may reach another device: no remote copies, remote signals or barrier semaphores. Data moves between devices by JAX's collectives and lax.ppermute only.
A program may use at most 64 MiB of HBM per device.

v0:
```python
import jax
import jax.numpy as jnp
from jax import lax
from jax.sharding import Mesh
from jax.sharding import PartitionSpec as P

ROW = ("row_0", "row_1")
ROW_COL = ("row_0", "row_1", "col")


def filled_up(lines, devices):
    spare = -len(lines) % devices
    return jnp.pad(lines, [(0, spare)] + [(0, 0)] * (lines.ndim - 1))


def spread(array, axis, root):
    lines = jnp.where(lax.axis_index(axis) == root, array, jnp.zeros_like(array)).reshape(
        -1, *array.shape[1:][-1:]
    )
    padded = filled_up(lines, lax.axis_size(axis))
    own = lax.psum_scatter(padded, axis, scatter_dimension=0, tiled=True)
    return lax.all_gather(own, axis, axis=0, tiled=True)[: len(lines)].reshape(array.shape)


def broadcast_by_axis(array, axes, root):
    array = jnp.where(lax.axis_index(axes) == root, array, jnp.zeros_like(array))
    for axis in axes:
        array = lax.psum(array, axis)
    return array


def in_blocks(array, dim, devices):
    before, after = (array.shape[:dim], array.shape[dim + 1 :])
    return jnp.moveaxis(array.reshape(*before, devices, -1, *after), dim, 0)


def sent_and_summed(array, axis, dim):
    pieces = in_blocks(array, dim, lax.axis_size(axis))
    arrived = lax.all_to_all(pieces, axis, split_axis=0, concat_axis=0, tiled=True)
    return arrived.astype(jnp.float32).sum(axis=0)


def multiply(left_tiles, left_columns, right_tiles, right_columns, target_columns, start_row):
    is_live = left_columns >= 0
    inner_rows = jnp.where(is_live, left_columns - start_row, 0).astype(jnp.int32)
    inner_columns = right_columns[inner_rows]
    matches = (
        (inner_columns[:, :, None, :] == target_columns[:, None, :, None])
        & is_live[:, :, None, None]
        & (target_columns >= 0)[:, None, :, None]
    )
    slot_index = jnp.argmax(matches.astype(jnp.int32), axis=-1)
    located = jnp.any(matches, axis=-1)
    selected = right_tiles[inner_rows[:, :, None], slot_index]
    selected = jnp.where(located[:, :, :, None, None], selected, jnp.zeros((), jnp.bfloat16))
    return jnp.einsum("iarc,iascd->isrd", left_tiles, selected, preferred_element_type=jnp.float32)


def on_device(density_tiles, tile_columns):
    row_count = lax.axis_size(ROW)
    column_count = lax.axis_size("col")
    layer_count = lax.axis_size("layer")
    grid_tiles, grid_columns = (
        lax.all_to_all(density_tiles, "col", split_axis=1, concat_axis=0, tiled=True),
        lax.all_to_all(tile_columns, "col", split_axis=1, concat_axis=0, tiled=True),
    )
    block_tiles = grid_tiles[:, 0]
    block_columns = grid_columns[:, 0]
    group_rows = block_tiles.shape[0]
    row_ratio = column_count // row_count
    panel_rows = group_rows // row_ratio
    per_layer = column_count // layer_count
    layer_index = lax.axis_index("layer")
    partial_value = jnp.zeros(block_tiles.shape, jnp.float32)
    for panel_step in range(per_layer):
        panel_index = layer_index * per_layer + panel_step
        left_tiles, left_columns = (
            spread(block_tiles, "col", panel_index),
            spread(block_columns, "col", panel_index),
        )
        right_tiles, right_columns = (
            broadcast_by_axis(block_tiles, ROW, panel_index // row_ratio),
            broadcast_by_axis(block_columns, ROW, panel_index // row_ratio),
        )
        partial_value = partial_value + multiply(
            left_tiles,
            left_columns,
            right_tiles,
            right_columns,
            block_columns,
            panel_index * panel_rows,
        )
    rounded = partial_value.astype(jnp.bfloat16)
    summed = sent_and_summed(rounded.astype(jnp.float32).astype(jnp.bfloat16), "layer", 2)
    returned = lax.all_to_all(
        summed.astype(jnp.bfloat16)[:, None], "col", split_axis=0, concat_axis=1, tiled=True
    )
    return returned


def solution(mesh):
    split = Mesh(
        mesh.devices.reshape(4, 2, mesh.shape["col"], mesh.shape["layer"]),
        ("row_0", "row_1", "col", "layer"),
    )
    return jax.shard_map(
        on_device,
        mesh=split,
        in_specs=(P(ROW_COL, None, None, None, None), P(ROW_COL, None, None)),
        out_specs=P(ROW_COL, None, None, "layer", None),
        check_vma=False,
    )
```

profile of v0, /device:TPU:1, one launch (start us, length us, event | category | flops | bytes accessed | tf_op | source)
XLA Modules:
  0.0 319.0 jit_solution(11141987187466286460)
XLA Ops:
  7.4 2.7 copy.204
  10.1 10.0 %all-to-all-start.1 = ((bf16[3,8,2,128,128]{4,3,2,0,1:T(8,128)(2,1)}), bf16[3,8,2,128,128]{4,3,2,0,1:T(8,128)(2,1)S(1)}, u32[]{:S(2)}, u32[]{:S(2)}) async-start(bf16[3,8,2,128,128]{4,3,2,0,1:T(8,128)(2,1)} %copy.204), calls=%async_computation.1 | async-start | bytes 3145728 | tf_op jit(solution)/shard_map/all_to_all | solution.py:64
  20.1 33.3 %all-to-all-done.1 = bf16[3,8,2,128,128]{4,3,2,0,1:T(8,128)(2,1)S(1)} async-done(((bf16[3,8,2,128,128]{4,3,2,0,1:T(8,128)(2,1)}), bf16[3,8,2,128,128]{4,3,2,0,1:T(8,128)(2,1)S(1)}, u32[]{:S(2)}, u32[]{:S(2)}) %all-to-all-start.1) | async-done | bytes 1572896 | tf_op jit(solution)/shard_map/all_to_all | solution.py:64
  53.4 2.8 broadcast_select_fusion.2
  56.3 0.5 reduce-scatter.5.cloned.1.call-update
  56.8 0.5 reduce-scatter.3.cloned.1.call-update
  57.4 82.9 %all-reduce.10.cloned.1.call-done = (bf16[24,2,128,128]{3,2,1,0:T(8,128)(2,1)}, bf16[24,2,128,128]{3,2,1,0:T(8,128)(2,1)}) async-done(((bf16[24,2,128,128]{3,2,1,0:T(8,128)(2,1)}, bf16[24,2,128,128]{3,2,1,0:T(8,128)(2,1)}), (bf16[24,2,128,128]{3,2,1,0:T(8,128)(2,1)}, bf16[24,2,128,128]{3,2,1,0:T(8,128)(2,1)})) %all-reduce.10.cloned.1.call-update) | async-done | bytes 3145744 | tf_op jit(solution)/shard_map/psum | solution.py:28
  140.4 0.5 all-gather.7.cloned.1.call-update
  140.9 0.1 copy-done
  141.0 0.7 copy.187
  141.7 7.8 %all-to-all-start = ((s32[3,8,2]{0,2,1:T(2,128)}), s32[3,8,2]{0,2,1:T(2,128)S(1)}, u32[]{:S(2)}, u32[]{:S(2)}) async-start(s32[3,8,2]{0,2,1:T(2,128)} %copy.187), calls=%async_computation | async-start | bytes 16384 | tf_op jit(solution)/shard_map/all_to_all | solution.py:65
  149.5 0.6 dynamic-slice
  150.7 5.9 %all-to-all-done = s32[3,8,2]{0,2,1:T(2,128)S(1)} async-done(((s32[3,8,2]{0,2,1:T(2,128)}), s32[3,8,2]{0,2,1:T(2,128)S(1)}, u32[]{:S(2)}, u32[]{:S(2)}) %all-to-all-start) | async-done | bytes 224 | tf_op jit(solution)/shard_map/all_to_all | solution.py:65
  156.6 0.1 squeeze.4
  156.7 0.1 copy.190
  156.8 25.1 %all-reduce.2 = (s32[24,2]{1,0:T(8,128)S(1)}, s32[24,2]{1,0:T(8,128)S(1)}) all-reduce(s32[24,2]{1,0:T(8,128)S(1)} %get-tuple-element.32, s32[24,2]{1,0:T(8,128)S(1)} %get-tuple-element.34), channel_id=4, replica_groups=mesh['row_0'=4,'row_1'=2,'col'=8,'layer'=4] {'col'}, use_global_device_ids=true, to_apply=%region_10.11.clone | all-reduce | flops 96 | bytes 768
  181.9 0.1 copy.192
  182.0 12.9 %all-gather = s32[8,3,2]{1,2,0:T(2,128)S(1)} all-gather(s32[1,3,2]{1,2,0:T(2,128)S(1)} %bitcast.110), channel_id=1, replica_groups=mesh['row_0'=4,'row_1'=2,'col'=8,'layer'=4] {'col'}, dimensions={0}, use_global_device_ids=true | all-gather | bytes 216 | tf_op jit(solution)/shard_map/all_gather | solution.py:22
  194.9 0.1 copy.193
  195.1 0.1 copy.202
  195.2 0.1 copy.210
  195.3 0.1 copy.194
  195.4 0.1 reshape.112
  195.5 0.1 copy.197
  195.6 0.1 copy.196
  195.6 0.1 reshape.114
  195.7 13.0 %all-gather.1 = s32[8,3,2]{1,2,0:T(2,128)S(1)} all-gather(s32[1,3,2]{1,2,0:T(2,128)S(1)} %bitcast.109), channel_id=1, replica_groups=mesh['row_0'=4,'row_1'=2,'col'=8,'layer'=4] {'col'}, dimensions={0}, use_global_device_ids=true | all-gather | bytes 216 | tf_op jit(solution)/shard_map/all_gather | solution.py:22
  208.7 0.1 copy.211
  208.8 0.1 copy.212
  208.9 0.1 reshape.116
  209.0 0.1 copy.215
  209.1 0.1 copy.214
  209.2 0.1 reshape.118
  209.3 0.1 copy.216
  209.4 0.1 copy.220
  209.5 0.1 reshape.81
  209.6 13.5 %all-reduce.3 = (s32[24,2]{1,0:T(8,128)S(1)}, s32[24,2]{1,0:T(8,128)S(1)}) all-reduce(s32[24,2]{1,0:T(8,128)S(1)} %get-tuple-element.33, s32[24,2]{1,0:T(8,128)S(1)} %get-tuple-element.31), channel_id=1, replica_groups=mesh['row_0'=4,'row_1'=2,'col'=8,'layer'=4] {'row_0'}, use_global_device_ids=true, to_apply=%region_8.9 | all-reduce | flops 96 | bytes 768 | tf_op jit(solution)/shard_map/psum | solution.py:28
  223.0 7.7 %all-reduce.4 = (s32[24,2]{1,0:T(8,128)S(1)}, s32[24,2]{1,0:T(8,128)S(1)}) all-reduce(s32[24,2]{1,0:T(8,128)S(1)} %get-tuple-element.11, s32[24,2]{1,0:T(8,128)S(1)} %get-tuple-element.12), channel_id=1, replica_groups=mesh['row_0'=4,'row_1'=2,'col'=8,'layer'=4] {'row_1'}, use_global_device_ids=true, to_apply=%region_9.10 | all-reduce | flops 96 | bytes 768 | tf_op jit(solution)/shard_map/psum | solution.py:28
  230.7 0.6 gather_fusion.2
  231.3 0.1 copy.218
  231.4 0.1 copy.198
  231.5 0.1 copy.205
  231.6 0.1 reshape.67
  231.7 0.6 gather_fusion
  232.3 0.1 copy.200
  232.4 0.1 copy.203
  232.5 0.1 copy.219
  232.7 0.6 iota_reduce_fusion
  233.3 0.1 copy.221
  233.4 0.1 reshape.87
  233.5 0.6 iota_reduce_fusion.1
  234.2 0.1 copy.206
  234.3 0.1 reshape.73
  234.4 11.8 %all-reduce.12.cloned.1.call-done = (bf16[24,2,128,128]{3,2,1,0:T(8,128)(2,1)}, bf16[24,2,128,128]{3,2,1,0:T(8,128)(2,1)}) async-done(((bf16[24,2,128,128]{3,2,1,0:T(8,128)(2,1)}, bf16[24,2,128,128]{3,2,1,0:T(8,128)(2,1)}), (bf16[24,2,128,128]{3,2,1,0:T(8,128)(2,1)}, bf16[24,2,128,128]{3,2,1,0:T(8,128)(2,1)})) %all-reduce.12.cloned.1.call-update) | async-done | bytes 3145744 | tf_op jit(solution)/shard_map/psum | solution.py:28
  246.2 4.5 %gather_fusion.3 = bf16[96,128,128]{2,1,0:T(8,128)(2,1)} fusion(bf16[24,2,128,128]{3,2,1,0:T(8,128)(2,1)} %get-tuple-element.17, s32[96]{0:T(128)S(1)} %reshape.87), kind=kCustom, calls=%fused_computation.3 | custom fusion | bytes 6292224 | tf_op jit(solution)/shard_map/gather | solution.py:54
  250.6 3.0 gather_fusion.1
  253.7 4.8 %fusion.1 = f32[24,2,128,128,1]{2,3,1,4,0:T(8,128)} fusion(bf16[24,2,128,128,1]{3,2,4,1,0:T(8,128)(2,1)} %bitcast.105, bf16[24,2,2,128,128]{4,3,2,1,0:T(8,128)(2,1)} %bitcast.95, pred[24,2,2]{2,1,0:T(4,128)(4,1)S(1)} %copy.219), kind=kOutput, calls=%fused_computation.6 | convolution fusion | flops 404226048 | bytes 7864416 | tf_op jit(solution)/shard_map/iarc,iascd->isrd/dot_general | solution.py:56
  258.5 5.5 %all-gather.5.cloned.1.call-done = bf16[6144,128]{1,0:T(8,128)(2,1)} async-done(((bf16[768,128]{1,0:T(8,128)(2,1)}), bf16[6144,128]{1,0:T(8,128)(2,1)}) %all-gather.5.cloned.1.call-update) | async-done | bytes 1572880 | tf_op jit(solution)/shard_map/all_gather | solution.py:22
  263.9 3.0 fusion
  267.0 0.4 copy.235
  267.4 24.0 %all_to_all.47 = bf16[4,24,2,32,128]{4,3,2,1,0:T(8,128)(2,1)S(1)} all-to-all(bf16[4,24,2,32,128]{4,3,2,1,0:T(8,128)(2,1)S(1)} %bitcast.97), channel_id=1, replica_groups=mesh['row_0'=4,'row_1'=2,'col'=8,'layer'=4] {'layer'}, dimensions={0} | all-to-all | bytes 3145728 | tf_op jit(solution)/shard_map/all_to_all | solution.py:39
  291.4 0.3 reduce_sum.12
  291.8 18.9 %all_to_all.48 = bf16[24,1,2,32,128]{4,3,2,1,0:T(8,128)(2,1)S(1)} all-to-all(bf16[24,1,2,32,128]{4,3,2,1,0:T(8,128)(2,1)S(1)} %bitcast.104), channel_id=1, replica_groups=mesh['row_0'=4,'row_1'=2,'col'=8,'layer'=4] {'col'}, dimensions={0} | all-to-all | bytes 786432 | tf_op jit(solution)/shard_map/all_to_all | solution.py:95
  310.6 0.8 copy.224
  (30 shorter events, 0.4 us)
Async XLA Ops:
  10.1 43.3 %all-to-all-start.1 = ((bf16[3,8,2,128,128]{4,3,2,0,1:T(8,128)(2,1)}), bf16[3,8,2,128,128]{4,3,2,0,1:T(8,128)(2,1)S(1)}, u32[]{:S(2)}, u32[]{:S(2)}) async-start(bf16[3,8,2,128,128]{4,3,2,0,1:T(8,128)(2,1)} %copy.204), calls=%async_computation.1 | async-start | bytes 3145728 | tf_op jit(solution)/shard_map/all_to_all | solution.py:64
  20.1 120.3 %all-reduce.10.cloned.1.call-start = ((), (), s32[]{:S(2)}) async-start(), calls=%async_computation.10 | async-start | bytes 6291456 | tf_op jit(solution)/shard_map/psum | solution.py:28
  56.2 84.2 %reduce-scatter.5.cloned.1.call-start = ((), (), s32[]{:S(2)}) async-start(), calls=%async_computation.8 | async-start | bytes 1769472 | tf_op jit(solution)/shard_map/reduce_scatter | solution.py:21
  56.8 138.2 %reduce-scatter.3.cloned.1.call-start = ((), (), s32[]{:S(2)}) async-start(), calls=%async_computation.6 | async-start | bytes 1769472 | tf_op jit(solution)/shard_map/reduce_scatter | solution.py:21
  57.4 188.8 %all-reduce.12.cloned.1.call-start = ((), (), s32[]{:S(2)}) async-start(), calls=%async_computation.11 | async-start | bytes 6291456 | tf_op jit(solution)/shard_map/psum | solution.py:28
  140.3 0.7 copy-start
  140.3 9.2 %copy-start.1 = (u32[256]{0:T(256)S(1)}, u32[256]{0:T(256)}, u32[]{:S(2)}) copy-start(u32[256]{0:T(256)} %constant.100) | copy-start | bytes 3076
  140.3 113.3 %all-gather.7.cloned.1.call-start = ((), (), s32[]{:S(2)}) async-start(), calls=%async_computation.9 | async-start | bytes 1769472 | tf_op jit(solution)/shard_map/all_gather | solution.py:22
  141.7 14.9 %all-to-all-start = ((s32[3,8,2]{0,2,1:T(2,128)}), s32[3,8,2]{0,2,1:T(2,128)S(1)}, u32[]{:S(2)}, u32[]{:S(2)}) async-start(s32[3,8,2]{0,2,1:T(2,128)} %copy.187), calls=%async_computation | async-start | bytes 16384 | tf_op jit(solution)/shard_map/all_to_all | solution.py:65
  149.5 114.4 %all-gather.5.cloned.1.call-start = ((), (), s32[]{:S(2)}) async-start(), calls=%async_computation.7 | async-start | bytes 1769472 | tf_op jit(solution)/shard_map/all_gather | solution.py:22
Sparse Core Ops, SparseCore 0:
  56.3 83.9 all-reduce.9
  143.0 103.1 all-reduce.11
Sparse Core Ops, SparseCore 1:
  59.3 43.9 reduce-scatter.4
  105.7 40.1 reduce-scatter.2
  147.6 63.6 all-gather.6
  213.1 50.8 all-gather.4
where the time goes:
time: 319 us
  waiting for transfers between devices  141 us (44%)
  blocking collectives  115 us (36%)
  starting transfers between devices  18 us (6%)
  local copies, waits for them, and re-layouts  16.9 us (5%)
  between operations  15.8 us (5%)
  matrix products  7.82 us (2%)
  other arithmetic  4.51 us (1%)
    psum x2, waiting for transfers between devices, broadcast_by_axis(): array = lax.psum(array, axis)  94.7 us
    all_to_all x1, waiting for transfers between devices, on_device(): lax.all_to_all(density_tiles, 'col', split_axis=1, concat_axis=0, tiled=T...  33.3 us
    all_gather x2, blocking collectives, spread(): lax.all_gather(own, axis, axis=0, tiled=True)[:len(lines)]  25.9 us
    unnamed x1, blocking collectives  25.1 us
    all_to_all x1, blocking collectives, sent_and_summed(): lax.all_to_all(pieces, axis, split_axis=0, concat_axis=0, tiled=True)  24 us
    psum x2, blocking collectives, broadcast_by_axis(): array = lax.psum(array, axis)  21.2 us
    all_to_all x1, blocking collectives, on_device(): lax.all_to_all(summed.astype(jnp.bfloat16)[:, None], 'col', split_axis=0,...  18.9 us
    all_to_all x1, starting transfers between devices, on_device(): lax.all_to_all(density_tiles, 'col', split_axis=1, concat_axis=0, tiled=T...  9.95 us
  transfers between devices with their start and end apart: 8, of which 5 were waited for; matrix products, arithmetic and copies ran while one was open for 6% of the time, Pallas kernels for 0%

commit v1 on v0

--- a/solution.py
+++ b/solution.py
@@ -6,6 +6,13 @@
 
 ROW = ("row_0", "row_1")
 ROW_COL = ("row_0", "row_1", "col")
+
+
+def gather_over(x, mesh_axis, dim):
+    n_dev = lax.axis_size(mesh_axis)
+    blocks = jnp.stack([x for _ in range(n_dev)])
+    blocks = lax.all_to_all(blocks, mesh_axis, split_axis=0, concat_axis=0)
+    return jnp.concatenate(blocks, axis=dim)
 
 
 def filled_up(lines, devices):
@@ -19,7 +26,7 @@
     )
     padded = filled_up(lines, lax.axis_size(axis))
     own = lax.psum_scatter(padded, axis, scatter_dimension=0, tiled=True)
-    return lax.all_gather(own, axis, axis=0, tiled=True)[: len(lines)].reshape(array.shape)
+    return gather_over(own, axis, 0)[: len(lines)].reshape(array.shape)
 
 
 def broadcast_by_axis(array, axes, root):

time: 319 us -> 351 us (1.10)
  starting transfers between devices: 18 us -> 41.7 us
  local copies, waits for them, and re-layouts: 16.9 us -> 22.1 us
    all_gather x2 -> x0, blocking collectives: 25.9 us -> none  [spread(): lax.all_gather(own, axis, axis=0, tiled=True)[:len(lines)]]
    all_to_all x0 -> x3, starting transfers between devices: none -> 21.5 us  [gather_over(): blocks = lax.all_to_all(blocks, mesh_axis, split_axis=0, concat_axis=0)]
    psum x2, blocking collectives: 21.2 us -> 39.1 us  [broadcast_by_axis(): array = lax.psum(array, axis)]
    all_to_all x0 -> x1, blocking collectives: none -> 10.1 us  [gather_over(): blocks = lax.all_to_all(blocks, mesh_axis, split_axis=0, concat_axis=0)]
    all_to_all x0 -> x3, waiting for transfers between devices: none -> 6.95 us  [gather_over(): blocks = lax.all_to_all(blocks, mesh_axis, split_axis=0, concat_axis=0)]
    all_gather x2 -> x0, waiting for transfers between devices: 5.51 us -> none  [spread(): lax.all_gather(own, axis, axis=0, tiled=True)[:len(lines)]]
    another operation x0 -> x4, local copies, waits for them, and re-layouts: none -> 5.48 us  [gather_over(): blocks = jnp.stack([x for _ in range(n_dev)])]
  transfers between devices with their start and end apart: 8 -> 9, of which waited for: 5 -> 5; matrix products, arithmetic and copies ran while one was open for 6% -> 7% of each run, Pallas kernels for 0% -> 0%
where the time goes in v1:
time: 351 us; the launch traced here: 350 us
  waiting for transfers between devices  140 us (40%)
  blocking collectives  118 us (34%)
  starting transfers between devices  41.7 us (12%)
  local copies, waits for them, and re-layouts  22.1 us (6%)
  between operations  15.6 us (4%)
  matrix products  7.71 us (2%)
  other arithmetic  4.49 us (1%)
    psum x2, waiting for transfers between devices, broadcast_by_axis(): array = lax.psum(array, axis)  93 us
    psum x2, blocking collectives, broadcast_by_axis(): array = lax.psum(array, axis)  39.1 us
    all_to_all x1, waiting for transfers between devices, on_device(): lax.all_to_all(density_tiles, 'col', split_axis=1, concat_axis=0, tiled=T...  33.3 us
    unnamed x1, blocking collectives  24.2 us
    all_to_all x1, blocking collectives, sent_and_summed(): lax.all_to_all(pieces, axis, split_axis=0, concat_axis=0, tiled=True)  23.4 us
    all_to_all x3, starting transfers between devices, gather_over(): blocks = lax.all_to_all(blocks, mesh_axis, split_axis=0, concat_axis=0)  21.5 us
    all_to_all x1, blocking collectives, on_device(): lax.all_to_all(summed.astype(jnp.bfloat16)[:, None], 'col', split_axis=0,...  21.2 us
    all_to_all x1, starting transfers between devices, on_device(): lax.all_to_all(tile_columns, 'col', split_axis=1, concat_axis=0, tiled=True)  10.2 us
  transfers between devices with their start and end apart: 9, of which 5 were waited for; matrix products, arithmetic and copies ran while one was open for 7% of the time, Pallas kernels for 0%

profile of v1, /device:TPU:1, one launch (start us, length us, event | category | flops | bytes accessed | tf_op | source)
XLA Modules:
  0.0 350.0 jit_solution(2816164539885409346)
XLA Ops:
  7.4 2.7 copy.171
  10.1 10.0 %all-to-all-start.2 = ((bf16[3,8,2,128,128]{4,3,2,0,1:T(8,128)(2,1)}), bf16[3,8,2,128,128]{4,3,2,0,1:T(8,128)(2,1)S(1)}, u32[]{:S(2)}, u32[]{:S(2)}) async-start(bf16[3,8,2,128,128]{4,3,2,0,1:T(8,128)(2,1)} %copy.171), calls=%async_computation.2 | async-start | bytes 3145728 | tf_op jit(solution)/shard_map/all_to_all | solution.py:71
  20.1 33.3 %all-to-all-done.2 = bf16[3,8,2,128,128]{4,3,2,0,1:T(8,128)(2,1)S(1)} async-done(((bf16[3,8,2,128,128]{4,3,2,0,1:T(8,128)(2,1)}), bf16[3,8,2,128,128]{4,3,2,0,1:T(8,128)(2,1)S(1)}, u32[]{:S(2)}, u32[]{:S(2)}) %all-to-all-start.2) | async-done | bytes 1572896 | tf_op jit(solution)/shard_map/all_to_all | solution.py:71
  53.4 2.8 broadcast_select_fusion.2
  56.3 0.5 all-reduce.10.cloned.1.call-update
  56.9 0.7 reduce-scatter.3.cloned.1.call-update
  57.6 0.7 copy.157
  58.3 10.2 %all-to-all-start = ((s32[3,8,2]{0,2,1:T(2,128)}), s32[3,8,2]{0,2,1:T(2,128)S(1)}, u32[]{:S(2)}, u32[]{:S(2)}) async-start(s32[3,8,2]{0,2,1:T(2,128)} %copy.157), calls=%async_computation | async-start | bytes 16384 | tf_op jit(solution)/shard_map/all_to_all | solution.py:72
  68.5 0.6 dynamic-slice
  69.6 5.9 %all-to-all-done = s32[3,8,2]{0,2,1:T(2,128)S(1)} async-done(((s32[3,8,2]{0,2,1:T(2,128)}), s32[3,8,2]{0,2,1:T(2,128)S(1)}, u32[]{:S(2)}, u32[]{:S(2)}) %all-to-all-start) | async-done | bytes 224 | tf_op jit(solution)/shard_map/all_to_all | solution.py:72
  75.5 0.1 squeeze.4
  75.6 0.1 copy.160
  75.7 24.2 %all-reduce.2 = (s32[24,2]{1,0:T(8,128)S(1)}, s32[24,2]{1,0:T(8,128)S(1)}) all-reduce(s32[24,2]{1,0:T(8,128)S(1)} %get-tuple-element.34, s32[24,2]{1,0:T(8,128)S(1)} %get-tuple-element.36), channel_id=4, replica_groups=mesh['row_0'=4,'row_1'=2,'col'=8,'layer'=4] {'col'}, use_global_device_ids=true, to_apply=%region_10.11.clone | all-reduce | flops 96 | bytes 768
  99.9 0.1 copy.162
  100.0 0.6 stack.8
  100.6 8.8 %all-to-all-start.1 = ((s32[8,3,2]{1,2,0:T(2,128)}), s32[8,3,2]{1,2,0:T(2,128)S(1)}, u32[]{:S(2)}, u32[]{:S(2)}) async-start(s32[8,3,2]{1,2,0:T(2,128)} %stack.8), calls=%async_computation.1 | async-start | bytes 16384 | tf_op jit(solution)/shard_map/all_to_all | solution.py:14
  109.4 0.1 copy.180
  109.5 6.9 %all-to-all-done.1 = s32[8,3,2]{1,2,0:T(2,128)S(1)} async-done(((s32[8,3,2]{1,2,0:T(2,128)}), s32[8,3,2]{1,2,0:T(2,128)S(1)}, u32[]{:S(2)}, u32[]{:S(2)}) %all-to-all-start.1) | async-done | bytes 224 | tf_op jit(solution)/shard_map/all_to_all | solution.py:14
  116.5 10.1 %all_to_all.67 = s32[8,3,2]{1,2,0:T(2,128)S(1)} all-to-all(s32[8,3,2]{1,2,0:T(2,128)S(1)} %stack.10), channel_id=1, replica_groups=mesh['row_0'=4,'row_1'=2,'col'=8,'layer'=4] {'col'}, dimensions={0} | all-to-all | bytes 384 | tf_op jit(solution)/shard_map/all_to_all | solution.py:14
  126.6 2.4 stack.11
  128.9 4.2 %all-to-all-start.5 = ((bf16[8,768,128]{2,1,0:T(8,128)(2,1)}), bf16[8,768,128]{2,1,0:T(8,128)(2,1)S(1)}, u32[]{:S(2)}, u32[]{:S(2)}) async-start(bf16[8,768,128]{2,1,0:T(8,128)(2,1)} %stack.11), calls=%async_computation.7 | async-start | bytes 3145728 | tf_op jit(solution)/shard_map/all_to_all | solution.py:14
  133.1 9.7 %all-reduce.10.cloned.1.call-done = (bf16[24,2,128,128]{3,2,1,0:T(8,128)(2,1)}, bf16[24,2,128,128]{3,2,1,0:T(8,128)(2,1)}) async-done(((bf16[24,2,128,128]{3,2,1,0:T(8,128)(2,1)}, bf16[24,2,128,128]{3,2,1,0:T(8,128)(2,1)}), (bf16[24,2,128,128]{3,2,1,0:T(8,128)(2,1)}, bf16[24,2,128,128]{3,2,1,0:T(8,128)(2,1)})) %all-reduce.10.cloned.1.call-update) | async-done | bytes 3145744 | tf_op jit(solution)/shard_map/psum | solution.py:35
  142.9 0.1 copy.169
  143.0 12.7 %all-reduce.3 = (s32[24,2]{1,0:T(8,128)S(1)}, s32[24,2]{1,0:T(8,128)S(1)}) all-reduce(s32[24,2]{1,0:T(8,128)S(1)} %get-tuple-element.35, s32[24,2]{1,0:T(8,128)S(1)} %get-tuple-element.33), channel_id=1, replica_groups=mesh['row_0'=4,'row_1'=2,'col'=8,'layer'=4] {'row_0'}, use_global_device_ids=true, to_apply=%region_8.9 | all-reduce | flops 96 | bytes 768 | tf_op jit(solution)/shard_map/psum | solution.py:35
  155.7 26.4 %all-reduce.4 = (s32[24,2]{1,0:T(8,128)S(1)}, s32[24,2]{1,0:T(8,128)S(1)}) all-reduce(s32[24,2]{1,0:T(8,128)S(1)} %get-tuple-element.11, s32[24,2]{1,0:T(8,128)S(1)} %get-tuple-element.12), channel_id=1, replica_groups=mesh['row_0'=4,'row_1'=2,'col'=8,'layer'=4] {'row_1'}, use_global_device_ids=true, to_apply=%region_9.10 | all-reduce | flops 96 | bytes 768 | tf_op jit(solution)/shard_map/psum | solution.py:35
  182.1 0.1 select_n.187
  182.2 2.5 stack.9
  184.7 8.5 %all-to-all-start.3 = ((bf16[8,768,128]{2,1,0:T(8,128)(2,1)}), bf16[8,768,128]{2,1,0:T(8,128)(2,1)}, u32[]{:S(2)}, u32[]{:S(2)}) async-start(bf16[8,768,128]{2,1,0:T(8,128)(2,1)} %stack.9), calls=%async_computation.4 | async-start | bytes 3145728 | tf_op jit(solution)/shard_map/all_to_all | solution.py:14
  193.2 0.1 ge.49
  193.3 0.1 copy.164
  193.4 0.1 reshape.167
  193.5 0.6 gather_fusion
  194.1 0.1 copy.166
  194.2 0.1 ge.52
  194.3 0.1 select_n.208
  194.4 0.1 copy.182
  194.5 0.1 reshape.181
  194.6 0.6 gather_fusion.2
  195.2 0.1 copy.184
  195.3 0.1 copy.188
  195.4 0.1 sub.48
  195.4 0.1 copy.189
  195.6 0.1 copy.173
  195.8 0.6 iota_reduce_fusion
  196.4 0.1 copy.191
  196.5 0.1 reshape.187
  196.7 0.1 copy.186
  196.8 0.1 sub.45
  196.9 0.1 copy.174
  197.0 0.1 copy.175
  197.0 0.6 iota_reduce_fusion.1
  197.7 0.1 copy.176
  197.8 0.1 reshape.173
  197.9 0.1 copy.170
  198.0 83.3 %all-reduce.12.cloned.1.call-done = (bf16[24,2,128,128]{3,2,1,0:T(8,128)(2,1)}, bf16[24,2,128,128]{3,2,1,0:T(8,128)(2,1)}) async-done(((bf16[24,2,128,128]{3,2,1,0:T(8,128)(2,1)}, bf16[24,2,128,128]{3,2,1,0:T(8,128)(2,1)}), (bf16[24,2,128,128]{3,2,1,0:T(8,128)(2,1)}, bf16[24,2,128,128]{3,2,1,0:T(8,128)(2,1)})) %all-reduce.12.cloned.1.call-update) | async-done | bytes 3145744 | tf_op jit(solution)/shard_map/psum | solution.py:35
  281.3 4.5 %gather_fusion.3 = bf16[96,128,128]{2,1,0:T(8,128)(2,1)} fusion(bf16[24,2,128,128]{3,2,1,0:T(8,128)(2,1)} %get-tuple-element.17, s32[96]{0:T(128)S(1)} %reshape.187), kind=kCustom, calls=%fused_computation.3 | custom fusion | bytes 6292224 | tf_op jit(solution)/shard_map/gather | solution.py:61
  285.8 2.9 gather_fusion.1
  288.7 4.7 %fusion.1 = f32[24,2,128,128,1]{2,3,1,4,0:T(8,128)} fusion(bf16[24,2,128,128,1]{3,2,4,1,0:T(8,128)(2,1)} %bitcast.104, bf16[24,2,2,128,128]{4,3,2,1,0:T(8,128)(2,1)} %bitcast.101, pred[24,2,2]{2,1,0:T(4,128)(4,1)S(1)} %copy.186), kind=kOutput, calls=%fused_computation.6 | convolution fusion | flops 404226048 | bytes 7864416 | tf_op jit(solution)/shard_map/iarc,iascd->isrd/dot_general | solution.py:63
  293.4 3.0 fusion
  296.5 0.4 copy.205
  296.9 23.4 %all_to_all.68 = bf16[4,24,2,32,128]{4,3,2,1,0:T(8,128)(2,1)S(1)} all-to-all(bf16[4,24,2,32,128]{4,3,2,1,0:T(8,128)(2,1)S(1)} %bitcast.103), channel_id=1, replica_groups=mesh['row_0'=4,'row_1'=2,'col'=8,'layer'=4] {'layer'}, dimensions={0} | all-to-all | bytes 3145728 | tf_op jit(solution)/shard_map/all_to_all | solution.py:46
  320.3 0.3 reduce_sum.12
  320.6 21.2 %all_to_all.69 = bf16[24,1,2,32,128]{4,3,2,1,0:T(8,128)(2,1)S(1)} all-to-all(bf16[24,1,2,32,128]{4,3,2,1,0:T(8,128)(2,1)S(1)} %bitcast.110), channel_id=1, replica_groups=mesh['row_0'=4,'row_1'=2,'col'=8,'layer'=4] {'col'}, dimensions={0} | all-to-all | bytes 786432 | tf_op jit(solution)/shard_map/all_to_all | solution.py:102
  341.8 0.8 copy.194
  (39 shorter events, 0.4 us)
Async XLA Ops:
  10.1 43.3 %all-to-all-start.2 = ((bf16[3,8,2,128,128]{4,3,2,0,1:T(8,128)(2,1)}), bf16[3,8,2,128,128]{4,3,2,0,1:T(8,128)(2,1)S(1)}, u32[]{:S(2)}, u32[]{:S(2)}) async-start(bf16[3,8,2,128,128]{4,3,2,0,1:T(8,128)(2,1)} %copy.171), calls=%async_computation.2 | async-start | bytes 3145728 | tf_op jit(solution)/shard_map/all_to_all | solution.py:71
  20.1 106.5 %reduce-scatter.5.cloned.1.call-start = ((), (), s32[]{:S(2)}) async-start(), calls=%async_computation.11 | async-start | bytes 1769472 | tf_op jit(solution)/shard_map/reduce_scatter | solution.py:28
  56.2 86.6 %all-reduce.10.cloned.1.call-start = ((), (), s32[]{:S(2)}) async-start(), calls=%async_computation.12 | async-start | bytes 6291456 | tf_op jit(solution)/shard_map/psum | solution.py:35
  56.8 0.8 copy-start.1
  56.8 11.7 %copy-start.2 = (u32[256]{0:T(256)S(1)}, u32[256]{0:T(256)}, u32[]{:S(2)}) copy-start(u32[256]{0:T(256)} %constant.100) | copy-start | bytes 3076
  56.8 125.3 %reduce-scatter.3.cloned.1.call-start = ((), (), s32[]{:S(2)}) async-start(), calls=%async_computation.10 | async-start | bytes 1769472 | tf_op jit(solution)/shard_map/reduce_scatter | solution.py:28
  58.3 17.3 %all-to-all-start = ((s32[3,8,2]{0,2,1:T(2,128)}), s32[3,8,2]{0,2,1:T(2,128)S(1)}, u32[]{:S(2)}, u32[]{:S(2)}) async-start(s32[3,8,2]{0,2,1:T(2,128)} %copy.157), calls=%async_computation | async-start | bytes 16384 | tf_op jit(solution)/shard_map/all_to_all | solution.py:72
  100.6 15.8 %all-to-all-start.1 = ((s32[8,3,2]{1,2,0:T(2,128)}), s32[8,3,2]{1,2,0:T(2,128)S(1)}, u32[]{:S(2)}, u32[]{:S(2)}) async-start(s32[8,3,2]{1,2,0:T(2,128)} %stack.8), calls=%async_computation.1 | async-start | bytes 16384 | tf_op jit(solution)/shard_map/all_to_all | solution.py:14
  128.9 53.2 %all-to-all-start.5 = ((bf16[8,768,128]{2,1,0:T(8,128)(2,1)}), bf16[8,768,128]{2,1,0:T(8,128)(2,1)S(1)}, u32[]{:S(2)}, u32[]{:S(2)}) async-start(bf16[8,768,128]{2,1,0:T(8,128)(2,1)} %stack.11), calls=%async_computation.7 | async-start | bytes 3145728 | tf_op jit(solution)/shard_map/all_to_all | solution.py:14
  133.1 148.2 %all-reduce.12.cloned.1.call-start = ((), (), s32[]{:S(2)}) async-start(), calls=%async_computation.13 | async-start | bytes 6291456 | tf_op jit(solution)/shard_map/psum | solution.py:35
  182.2 2.5 copy-start
  184.7 108.7 %all-to-all-start.3 = ((bf16[8,768,128]{2,1,0:T(8,128)(2,1)}), bf16[8,768,128]{2,1,0:T(8,128)(2,1)}, u32[]{:S(2)}, u32[]{:S(2)}) async-start(bf16[8,768,128]{2,1,0:T(8,128)(2,1)} %stack.9), calls=%async_computation.4 | async-start | bytes 3145728 | tf_op jit(solution)/shard_map/all_to_all | solution.py:14
Sparse Core Ops, SparseCore 0:
  56.3 44.0 reduce-scatter.4
  103.0 42.9 reduce-scatter.2
Sparse Core Ops, SparseCore 1:
  59.1 83.7 all-reduce.9
  145.3 135.9 all-reduce.11
